TPU v7x, 256 devices: a whole 4x4x8 slice. The times are simulated.
256 devices in a mesh: seg: 256 (over x, z, y, core).
Axes of the slice: x: 4, y: 4, z: 8, core: 2. Of those that a mesh axis runs over, the one named last changes fastest.
Arguments:
- cam_jac: bfloat16 [18, 4096, 512], P(None, 'seg'), may hold values from -0.25 to 0.25
- point_jac: bfloat16 [6, 4096, 512], P(None, 'seg'), may hold values from -6 to 6
- obs_point: int32 [4096, 512], P('seg'), may hold values from 0 to 1791, as said below
- obs_count: int32 [4096], P('seg'), may hold values from 64 to 512, as said below
- back_list: int32 [256, 384], P('seg'), may hold values from 0 to 1023, as said below
- front_list: int32 [256, 384], P('seg'), may hold values from 0 to 1023, as said below
- point_damp: float32 [262144], P('seg'), may hold values from 0.5 to 4
- cam_damp: float32 [4096], P('seg'), may hold values from 0.1 to 1
- right_side: float32 [9, 4096], P(None, 'seg'), may hold values from -25 to 25
- start_guess: float32 [9, 4096], P(None, 'seg'), may hold values from -3 to 3
Outputs:
- camera_step: float32 [9, 4096], P(None, 'seg')
- residual: float32 [9, 4096], P(None, 'seg')
Inputs may be any that keep to these rules, and one draw needn't show every extreme that they name: `obs_point`: entries below 1024 name the segment's own points; an entry e from 1024 to 1407 names entry e - 1024 of the previous segment's back_list, and a larger one entry e - 1408 of the next segment's front_list. Keyframes of the first segment name no back slot, those of the last segment no front slot. `obs_count`: slots at or past a keyframe's count are padding. Every segment has a keyframe whose slots are all used. `back_list`: each row holds 384 distinct own points of the segment; no point stands on both lists of its segment. `front_list`: each row holds 384 distinct own points of the segment; no point stands on both lists of its segment.
All inputs are finite; a program needn't handle non-finite values.
Results may differ from a plain program's by a relative error of at most 0.0005.
Values sent between devices are 32-bit elements; how exact they have to be, the bound alone decides.
No kernel may reach another device: no remote copies, remote signals or barrier semaphores. Data moves between devices by JAX's collectives and lax.ppermute only.
A program may use at most 64 MiB of HBM per device.

v0:
```python
import jax
import jax.numpy as jnp
from jax import lax
from jax.experimental import pallas as pl
from jax.experimental.pallas import tpu as pltpu
from jax.sharding import Mesh
from jax.sharding import PartitionSpec as P


F32 = jnp.float32
BF16 = jnp.bfloat16
I32 = jnp.int32
LANES = 128
ENTRY_PAIRS = ((0, 0), (0, 1), (0, 2), (1, 1), (1, 2), (2, 2))

SIDE = 6
NEXT_SLOTS = 3
PREV_SLOTS = 6
OWN_FRONT = 9
INTERIOR = 12
PAD_ROWS = 16


def row_of(block, index, rows):
    return jnp.broadcast_to(block[index : index + 1, :], (rows, block.shape[1]))


def sub_iota(rows, width):
    return lax.broadcasted_iota(I32, (rows, width), 0)


def lane_iota(rows, width):
    return lax.broadcasted_iota(I32, (rows, width), 1)


def nt(left, right, **kw):
    return lax.dot_general(
        left, right, (((1,), (1,)), ((), ())), preferred_element_type=F32, **kw
    )


def split_two(value):
    high = value.astype(BF16)
    low = (value - high.astype(F32)).astype(BF16)
    return high.astype(F32), low.astype(F32)


def flip_block(block_ref):
    return jnp.transpose(block_ref[...])[:16]


def one_hot_rows(index_row, rows, width):
    packed = jnp.broadcast_to(index_row, (16, width)).astype(BF16)
    parts = []
    for start in range(0, rows, 16):
        ids = (sub_iota(16, width) + start).astype(F32).astype(BF16)
        parts.append(jnp.where(packed == ids, jnp.ones_like(packed), jnp.zeros_like(packed)))
    return parts[0] if len(parts) == 1 else jnp.concatenate(parts, axis=0)


def scatter_rows(value_refs, high_ref, low_ref, cameras, width, group):
    ids = sub_iota(16, width).astype(F32).astype(BF16)

    def step(number, total):
        for inner in range(group):
            pick = pl.ds(number * group + inner, 1)
            lanes = one_hot_rows(low_ref[pick, :], LANES, width).astype(jnp.float8_e4m3fn)
            mask = jnp.broadcast_to(high_ref[pick, :], (16, width)).astype(BF16) == ids
            rows = []
            for ref, index in value_refs:
                spread = jnp.broadcast_to(ref[index, pick, :], (16, width)).astype(BF16)
                rows.append(jnp.where(mask, spread, jnp.zeros_like(spread)))
            piece = nt(jnp.concatenate(rows, axis=0), lanes)
            total = piece if total is None else total + piece
        return total

    if group == cameras:
        return step(0, None)
    start = jnp.zeros((16 * len(value_refs), LANES), F32)
    return lax.fori_loop(0, cameras // group, step, start)


def fold_parts(total, index):
    start = 2 * PAD_ROWS * index
    return total[start : start + PAD_ROWS] + total[start + PAD_ROWS : start + 2 * PAD_ROWS]


def gather_rows(tables, row_index, lane_index, rows):
    halves = []
    for top in range(0, row_index.shape[0], 8):
        pieces = []
        for start in range(0, row_index.shape[1], LANES):
            row_part = row_index[top : top + 8, start : start + LANES]
            lane_part = lane_index[top : top + 8, start : start + LANES]
            outs = [None] * len(tables)
            for row in range(rows):
                here = row_part == row
                for number, table in enumerate(tables):
                    spread = jnp.broadcast_to(table[row : row + 1, :], (8, LANES))
                    got = jnp.take_along_axis(spread, lane_part, axis=1, mode="promise_in_bounds")
                    outs[number] = got if row == 0 else jnp.where(here, got, outs[number])
            pieces.append(outs)
        halves.append([jnp.concatenate([p[n] for p in pieces], axis=1) for n in range(len(tables))])
    return [jnp.concatenate([h[n] for h in halves], axis=0) for n in range(len(tables))]


def errors_of(cam_ref, vector, weights):
    rows = []
    for row in range(2):
        running = None
        for column in range(9):
            term = cam_ref[9 * row + column].astype(F32) * vector[:, column : column + 1]
            running = term if running is None else running + term
        rows.append(running * weights)
    return rows


def send_rows(mate_ref, other_ref, index, block):
    odd = lax.axis_index("core") == 1
    to_next = block[:SIDE]
    to_prev = block[SIDE : 2 * SIDE]
    mate_ref[SIDE * index : SIDE * (index + 1), :] = jnp.where(odd, to_prev, to_next)
    other_ref[SIDE * index : SIDE * (index + 1), :] = jnp.where(odd, to_next, to_prev)


def point_table(back, front):
    border = back.shape[1]
    eight = sub_iota(8, border)
    lanes = lane_iota(8, border)
    lefts, rights = [], []
    for listed, base in ((back, 0), (front, OWN_FRONT)):
        high = listed >> 7
        low = listed & 127
        hit = jnp.broadcast_to(high, (8, border)) == eight
        row_value = ((lanes >> 7) + (base + 1)).astype(F32)
        lane_value = (lanes & 127).astype(F32)
        zero = jnp.zeros((8, border), F32)
        lefts.append(
            jnp.concatenate(
                [jnp.where(hit, row_value, zero), jnp.where(hit, lane_value, zero)], axis=0
            ).astype(BF16)
        )
        rights.append(one_hot_rows(low.astype(F32), LANES, border))
    table = nt(lefts[0], rights[0]) + nt(lefts[1], rights[1])
    row_plus = table[:8]
    lane = table[8:]
    free = jnp.where(row_plus == 0.0, 1.0, 0.0)
    upper = jnp.where(sub_iota(LANES, LANES) <= lane_iota(LANES, LANES), 1.0, 0.0).astype(BF16)
    seen = lax.dot_general(
        free.astype(BF16), upper, (((1,), (0,)), ((), ())), preferred_element_type=F32
    )
    total = jnp.broadcast_to(seen[:, LANES - 1 : LANES], (8, LANES))
    before = jnp.zeros((8, LANES), F32)
    rows = sub_iota(8, LANES)
    for row in range(7):
        before = before + jnp.where(rows > row, row_of(total, row, 8), 0.0)
    rank = before + seen - free
    return jnp.where(
        free > 0.0, rank + float(INTERIOR * LANES), (row_plus - 1.0) * float(LANES) + lane
    ).astype(I32)


def first_kernel(
    cam_hbm, point_hbm, obs_hbm, count_hbm, back_hbm, front_hbm, damp_hbm, cam_damp_hbm,
    right_hbm, guess_hbm,
    mate_ref, other_ref, own_ref, index_ref, errors_ref, jac_ref, state_ref,
    value_ref, high_ref, low_ref,
    cam_ref, point_ref, obs_ref, count_ref, back_ref, front_ref, damp_ref, cam_damp_ref,
    right_ref, guess_ref, flip_ref, sems,
):
    sources = (
        back_hbm, front_hbm, obs_hbm, guess_hbm, right_hbm, cam_damp_hbm, count_hbm, point_hbm,
        cam_hbm, damp_hbm,
    )
    targets = (
        back_ref, front_ref, obs_ref, guess_ref, right_ref, cam_damp_ref, count_ref, point_ref,
        cam_ref, damp_ref,
    )
    copies = [
        pltpu.make_async_copy(source, target, sems.at[number])
        for number, (source, target) in enumerate(zip(sources, targets))
    ]
    for copy in copies:
        copy.start()
    cameras, width = obs_ref.shape
    border = back_ref.shape[1]
    points = damp_ref.shape[0] * damp_ref.shape[1]
    for copy in copies[:2]:
        copy.wait()
    table = point_table(back_ref[...], front_ref[...])
    for copy in copies[2:7]:
        copy.wait()
    observed = obs_ref[...]
    own_place = gather_rows([table], observed >> 7, observed & 127, points // LANES)[0]
    place = jnp.where(
        observed < points,
        own_place,
        jnp.where(
            observed < points + border,
            observed + (PREV_SLOTS * LANES - points),
            observed + (NEXT_SLOTS * LANES - points - border),
        ),
    )
    index_ref[...] = place
    high_ref[...] = (place >> 7).astype(F32)
    low_ref[...] = (place & 127).astype(F32)
    valid = lane_iota(16, LANES) < 9
    flip_ref[0, :9, :16] = guess_ref[...]
    flip_ref[1, :9, :16] = right_ref[...]
    flip_ref[2, 0:1, :16] = cam_damp_ref[...]
    flip_ref[2, 1:2, :16] = count_ref[...].astype(F32)
    guess = jnp.where(valid, flip_block(flip_ref.at[0]), 0.0)
    right = jnp.where(valid, flip_block(flip_ref.at[1]), 0.0)
    sides = flip_block(flip_ref.at[2])
    damp = jnp.where(valid, sides[:, 0:1], 0.0)
    weights = (lane_iota(cameras, width).astype(F32) < sides[:, 1:2]).astype(F32)
    state_ref[0] = guess
    state_ref[1] = right
    state_ref[2] = damp
    copies[7].wait()
    jac = [point_ref[entry].astype(F32) * weights for entry in range(6)]
    for entry in range(6):
        jac_ref[entry] = jac[entry]
    jac_ref[6] = weights
    products = [jac[a] * jac[b] + jac[3 + a] * jac[3 + b] for a, b in ENTRY_PAIRS]
    copies[8].wait()
    copies[9].wait()
    ids = sub_iota(16, LANES).astype(F32).astype(BF16)
    damping = None
    new_high = (table >> 7).astype(F32)
    new_low = (table & 127).astype(F32)
    first, rest = split_two(damp_ref[...])
    last = damp_ref[...] - first - rest
    for row in range(points // LANES):
        lanes = one_hot_rows(new_low[row : row + 1, :], LANES, LANES)
        mask = row_of(new_high, row, 16).astype(BF16) == ids
        parts = []
        for part in (first, rest, last):
            spread = row_of(part, row, 16).astype(BF16)
            parts.append(jnp.where(mask, spread, jnp.zeros_like(spread)))
        piece = nt(jnp.concatenate(parts, axis=0), lanes)
        damping = piece if damping is None else damping + piece
    damping = damping[:16] + damping[16:32] + damping[32:]
    errors = errors_of(cam_ref, guess, weights)
    errors_ref[0] = errors[0]
    errors_ref[1] = errors[1]
    products += [errors[0] * jac[j] + errors[1] * jac[3 + j] for j in range(3)]
    for number, product in enumerate(products):
        value_ref[2 * number], value_ref[2 * number + 1] = split_two(product)
    total = scatter_rows(
        [(value_ref, number) for number in range(18)], high_ref, low_ref, cameras, width, 8
    )
    for number in range(9):
        block = fold_parts(total, number)
        if number in (0, 3, 5):
            block = block + damping
        own_ref[number] = block
        send_rows(mate_ref, other_ref, number, block)


def complete(own_ref, mate_ref, other_ref, number):
    odd = lax.axis_index("core") == 1
    block = own_ref[number]
    mate = mate_ref[SIDE * number : SIDE * (number + 1), :]
    other = other_ref[SIDE * number : SIDE * (number + 1), :]
    after = jnp.where(odd, other, mate)
    before = jnp.where(odd, mate, other)
    tail = jnp.zeros((PAD_ROWS - 2 * SIDE, LANES), F32)
    return block + jnp.concatenate([after, before, tail], axis=0)


def symmetric_inverse(entries):
    cofactors = [
        entries[3] * entries[5] - entries[4] * entries[4],
        entries[2] * entries[4] - entries[1] * entries[5],
        entries[1] * entries[4] - entries[2] * entries[3],
        entries[0] * entries[5] - entries[2] * entries[2],
        entries[1] * entries[2] - entries[0] * entries[4],
        entries[0] * entries[3] - entries[1] * entries[1],
    ]
    determinant = entries[0] * cofactors[0] + entries[1] * cofactors[1] + entries[2] * cofactors[2]
    determinant = jnp.where(determinant == 0.0, 1.0, determinant)
    return [member / determinant for member in cofactors]


def apply_inverse(inverse, sums):
    return [
        inverse[0] * sums[0] + inverse[1] * sums[1] + inverse[2] * sums[2],
        inverse[1] * sums[0] + inverse[3] * sums[1] + inverse[4] * sums[2],
        inverse[2] * sums[0] + inverse[4] * sums[1] + inverse[5] * sums[2],
    ]


def pack_columns(cols):
    lanes = lane_iota(16, LANES)
    out = jnp.zeros((16, LANES), F32)
    for number, col in enumerate(cols):
        out = jnp.where(lanes == number, col, out)
    return out


def gather_side(values, place, block_base, rows, extra):
    odd_base, even_base = block_base
    odd = lax.axis_index("core") == 1
    base = jnp.where(odd, odd_base, even_base)
    sides = [
        jnp.where(odd, v[odd_base : odd_base + rows], v[even_base : even_base + rows])
        for v in values
    ]
    lines = [([side[r : r + 1] for side in sides], base + r) for r in range(rows)]
    lines += [([v[r : r + 1] for v in values], r) for r in extra]
    halves = []
    for top in range(0, place.shape[0], 8):
        pieces = []
        for start in range(0, place.shape[1], LANES):
            part = place[top : top + 8, start : start + LANES]
            row_part = part >> 7
            lane_part = part & 127
            outs = [jnp.zeros((8, LANES), F32) for _ in values]
            for tables, number in lines:
                here = row_part == number
                for k, table in enumerate(tables):
                    spread = jnp.broadcast_to(table, (8, LANES))
                    got = jnp.take_along_axis(spread, lane_part, axis=1, mode="promise_in_bounds")
                    outs[k] = jnp.where(here, got, outs[k])
            pieces.append(outs)
        halves.append([jnp.concatenate([p[n] for p in pieces], axis=1) for n in range(3)])
    return [jnp.concatenate([h[n] for h in halves], axis=0) for n in range(3)]


def subtract_points(jac_ref, errors_ref, picked):
    return [
        errors_ref[row]
        - (
            picked[0] * jac_ref[3 * row]
            + picked[1] * jac_ref[3 * row + 1]
            + picked[2] * jac_ref[3 * row + 2]
        )
        for row in range(2)
    ]


def with_mate(own_ref, mate_ref, number):
    odd = lax.axis_index("core") == 1
    mate = mate_ref[SIDE * number : SIDE * (number + 1), :]
    none = jnp.zeros_like(mate)
    tail = jnp.zeros((PAD_ROWS - 2 * SIDE, LANES), F32)
    after = jnp.where(odd, none, mate)
    before = jnp.where(odd, mate, none)
    return own_ref[number] + jnp.concatenate([after, before, tail], axis=0)


def early_first_kernel(jac_ref, index_ref, errors_in, own_in, mate_in, left_ref):
    blocks = [with_mate(own_in, mate_in, number) for number in range(9)]
    values = apply_inverse(symmetric_inverse(blocks[:6]), blocks[6:])
    picked = gather_side(values, index_ref[...], (SIDE, 0), SIDE, (INTERIOR, INTERIOR + 1))
    left_ref[0], left_ref[1] = subtract_points(jac_ref, errors_in, picked)


def early_kernel(jac_ref, index_ref, errors_in, own_in, mate_in, inverse_in, left_ref):
    sums = [with_mate(own_in, mate_in, number) for number in range(3)]
    values = apply_inverse([inverse_in[number] for number in range(6)], sums)
    picked = gather_side(values, index_ref[...], (SIDE, 0), SIDE, (INTERIOR, INTERIOR + 1))
    left_ref[0], left_ref[1] = subtract_points(jac_ref, errors_in, picked)


def project(cam_ref, jac_ref, left_ref, values, place):
    picked = gather_side(values, place, (0, SIDE), SIDE, ())
    adjusted = subtract_points(jac_ref, left_ref, picked)
    cols = []
    for column in range(9):
        term = (
            cam_ref[column].astype(F32) * adjusted[0]
            + cam_ref[9 + column].astype(F32) * adjusted[1]
        )
        cols.append(jnp.sum(term, axis=1, keepdims=True))
    return pack_columns(cols)


def next_scatter(
    cam_ref, jac_ref, vector, place, value_ref, high_ref, low_ref,
    mate_ref, other_ref, own_ref, errors_ref,
):
    cameras, width = place.shape
    errors = errors_of(cam_ref, vector, jac_ref[6])
    errors_ref[0] = errors[0]
    errors_ref[1] = errors[1]
    for j in range(3):
        product = errors[0] * jac_ref[j] + errors[1] * jac_ref[3 + j]
        value_ref[2 * j], value_ref[2 * j + 1] = split_two(product)
    high_ref[...] = (place >> 7).astype(F32)
    low_ref[...] = (place & 127).astype(F32)
    total = scatter_rows(
        [(value_ref, number) for number in range(6)], high_ref, low_ref, cameras, width, 8
    )
    blocks = []
    for number in range(3):
        block = fold_parts(total, number)
        own_ref[number] = block
        send_rows(mate_ref, other_ref, number, block)
        blocks.append(block)
    return errors, blocks


def side_kernel(cam_ref, jac_ref, given, precond_ref):
    cols = []
    for column in range(9):
        squared = cam_ref[column].astype(F32) ** 2 + cam_ref[9 + column].astype(F32) ** 2
        cols.append(jnp.sum(squared * jac_ref[6], axis=1, keepdims=True))
    valid = lane_iota(16, LANES) < 9
    precond_ref[...] = jnp.where(valid, 1.0 / (pack_columns(cols) + given[2]), 0.0)


def second_kernel(
    cam_ref, jac_ref, index_ref, errors_in, own_in, mate_in, other_in, state_in, precond_in,
    mate_ref, other_ref, own_ref, errors_ref, inverse_ref, state_ref,
    value_ref, high_ref, low_ref,
):
    blocks = [complete(own_in, mate_in, other_in, number) for number in range(9)]
    inverse = symmetric_inverse(blocks[:6])
    for number in range(6):
        inverse_ref[number] = inverse[number]
    place = index_ref[...]
    values = apply_inverse(inverse, blocks[6:])
    image = project(cam_ref, jac_ref, errors_in, values, place)
    guess, right, damp = state_in[0], state_in[1], state_in[2]
    precond = precond_in[...]
    residual = right - (damp * guess + image)
    scaled = precond * residual
    state_ref[0] = residual
    state_ref[1] = scaled
    state_ref[2] = precond
    next_scatter(
        cam_ref, jac_ref, scaled, place, value_ref, high_ref, low_ref,
        mate_ref, other_ref, own_ref, errors_ref,
    )


def unshared_rows():
    chip = lax.axis_index("chip")
    core = lax.axis_index("core")
    first = jnp.logical_and(chip == 0, core == 0)
    last = jnp.logical_and(chip == lax.axis_size("chip") - 1, core == 1)
    start = jnp.where(first, SIDE, INTERIOR)
    stop = jnp.where(last, SIDE, 0)
    rows = sub_iota(PAD_ROWS, LANES)
    return jnp.logical_or(rows >= start, rows < stop)


def column_sums(block):
    return jnp.sum(block, axis=0, keepdims=True)


def third_kernel(
    cam_ref, jac_ref, index_ref, errors_in, own_in, mate_in, other_in, inverse_in, given, state_in,
    mate_ref, other_ref, own_ref, errors_ref, state_ref, rows_ref,
    value_ref, high_ref, low_ref,
):
    sums = [complete(own_in, mate_in, other_in, number) for number in range(3)]
    inverse = [inverse_in[number] for number in range(6)]
    values = apply_inverse(inverse, sums)
    place = index_ref[...]
    image = project(cam_ref, jac_ref, errors_in, values, place)
    damp = given[2]
    residual, scaled, precond = state_in[0], state_in[1], state_in[2]
    image = damp * scaled + image
    tilde_residual = residual - image
    tilde = precond * tilde_residual
    state_ref[0] = image
    state_ref[1] = tilde_residual
    state_ref[2] = tilde
    errors, blocks = next_scatter(
        cam_ref, jac_ref, tilde, place, value_ref, high_ref, low_ref,
        mate_ref, other_ref, own_ref, errors_ref,
    )
    energy = column_sums(damp * tilde * tilde)
    squares = column_sums(errors[0] * errors[0] + errors[1] * errors[1])
    for start in range(0, squares.shape[1], LANES):
        energy = energy + squares[:, start : start + LANES]
    lone = unshared_rows()
    for value, point in zip(apply_inverse(inverse, blocks), blocks):
        energy = energy - column_sums(jnp.where(lone, value * point, 0.0))
    rows = [
        column_sums(residual * scaled),
        column_sums(image * scaled),
        column_sums(tilde_residual * tilde),
        column_sums(image * tilde),
        column_sums(image * (precond * image)),
        energy,
    ]
    for number, row in enumerate(rows):
        rows_ref[number : number + 1, :] = row
        mate_ref[3 * SIDE + number : 3 * SIDE + number + 1, :] = row


def sum_kernel(own_in, mate_in, other_in, inverse_in, rows_in, values_ref, dots_ref):
    sums = [complete(own_in, mate_in, other_in, number) for number in range(3)]
    inverse = [inverse_in[number] for number in range(6)]
    values = apply_inverse(inverse, sums)
    shared = None
    for number in range(3):
        values_ref[number] = values[number]
        term = values[number] * sums[number]
        shared = term if shared is None else shared + term
    border = column_sums(jnp.where(unshared_rows(), 0.0, shared))
    rows = rows_in[...] + mate_in[3 * SIDE : 3 * SIDE + 6, :]
    rows = rows - jnp.where(sub_iota(6, LANES) == 5, border, 0.0)
    totals = jnp.sum(rows, axis=1, keepdims=True)
    line = column_sums(jnp.where(sub_iota(6, LANES) == lane_iota(6, LANES), totals, 0.0))
    dots_ref[...] = jnp.broadcast_to(line, dots_ref.shape)


def finish_kernel(
    cam_ref, jac_ref, index_ref, errors_in, values_in, given, state_in, tilde_in, dots_ref,
    step_ref, residual_ref, flip_ref,
):
    values = [values_in[number] for number in range(3)]
    image = project(cam_ref, jac_ref, errors_in, values, index_ref[...])
    guess, damp = given[0], given[2]
    scaled, precond = state_in[1], state_in[2]
    first, tilde_residual, tilde = (tilde_in[number] for number in range(3))
    image = damp * tilde + image
    total = column_sums(dots_ref[...])
    inner, curve, tilde_inner, cross, back_inner, tilde_curve = (
        total[:, number : number + 1] for number in range(6)
    )
    mixed = cross - tilde_curve
    back_curve = back_inner - mixed
    first_step = inner / curve
    shift = first_step - 1.0
    inner_next = tilde_inner - 2.0 * shift * cross + shift * shift * back_inner
    curve_next = tilde_curve - 2.0 * shift * mixed + shift * shift * back_curve
    ratio = inner_next / inner
    against = cross - shift * back_inner
    second_step = inner_next / (curve_next + 2.0 * ratio * against + ratio * ratio * curve)
    direction = tilde - shift * (precond * first) + ratio * scaled
    moved = image - shift * (first - image) + ratio * first
    flip_ref[0, :16, :] = guess + first_step * scaled + second_step * direction
    flip_ref[1, :16, :] = tilde_residual - shift * first - second_step * moved
    step_ref[...] = jnp.transpose(flip_ref[0])[:9, :16]
    residual_ref[...] = jnp.transpose(flip_ref[1])[:9, :16]


def vmem(count):
    return [pl.BlockSpec(memory_space=pltpu.VMEM) for _ in range(count)]


def out_f32(*shape):
    return jax.ShapeDtypeStruct(shape, F32)


SEG = ("chip", "core")


def shards(
    cam_jac, point_jac, obs_point, obs_count, back_list, front_list, point_damp, cam_damp,
    right_side, start_guess,
):
    cameras, width = obs_point.shape
    chips = lax.axis_size("chip")
    count = 2 * chips
    mates = [(i, i ^ 1) for i in range(count)]
    others = []
    for i in range(1, count - 1, 2):
        others += [(i, i + 1), (i + 1, i)]
    params = pltpu.CompilerParams(vmem_limit_bytes=16 * 2**20)
    inputs = (
        cam_jac, point_jac, obs_point, obs_count.reshape(1, -1), back_list, front_list,
        point_damp.reshape(-1, LANES), cam_damp.reshape(1, -1), right_side, start_guess,
    )

    def scratch(values):
        return [
            pltpu.VMEM((values, cameras, width), F32),
            pltpu.VMEM((cameras, width), F32),
            pltpu.VMEM((cameras, width), F32),
        ]

    def exchange(to_mate, to_other):
        other = lax.ppermute(to_other, SEG, others)
        mate = lax.ppermute(to_mate, SEG, mates)
        return mate, other

    def call(kernel, outs, operands, scratches=(), spaces=None):
        return pl.pallas_call(
            kernel,
            out_shape=outs,
            in_specs=spaces or vmem(len(operands)),
            out_specs=tuple(vmem(len(outs))),
            scratch_shapes=list(scratches),
            compiler_params=params,
        )(*operands)

    plane = out_f32(2, cameras, width)
    to_mate, to_other, own, place, errors, jac, given = call(
        first_kernel,
        (
            out_f32(9 * SIDE, LANES),
            out_f32(9 * SIDE, LANES),
            out_f32(9, PAD_ROWS, LANES),
            jax.ShapeDtypeStruct((cameras, width), I32),
            plane,
            out_f32(7, cameras, width),
            out_f32(3, 16, LANES),
        ),
        tuple(pltpu.with_memory_space_constraint(value, pltpu.HBM) for value in inputs),
        scratch(18)
        + [pltpu.VMEM(value.shape, value.dtype) for value in inputs]
        + [pltpu.VMEM((3, LANES, LANES), F32), pltpu.SemaphoreType.DMA((len(inputs),))],
        [pl.BlockSpec(memory_space=pltpu.HBM) for _ in inputs],
    )
    mate, other = exchange(to_mate, to_other)
    (precond,) = call(side_kernel, (out_f32(16, LANES),), (cam_jac, jac, given))
    (left,) = call(early_first_kernel, (plane,), (jac, place, errors, own, mate))
    own_shape = out_f32(3, PAD_ROWS, LANES)
    to_mate, to_other, own, errors, inverse, state = call(
        second_kernel,
        (
            out_f32(3 * SIDE, LANES),
            out_f32(3 * SIDE, LANES),
            own_shape,
            plane,
            out_f32(6, PAD_ROWS, LANES),
            out_f32(3, 16, LANES),
        ),
        (cam_jac, jac, place, left, own, mate, other, given, precond),
        scratch(6),
    )
    mate, other = exchange(to_mate, to_other)
    (left,) = call(early_kernel, (plane,), (jac, place, errors, own, mate, inverse))
    to_mate, to_other, own, errors, tilde, rows = call(
        third_kernel,
        (
            out_f32(3 * SIDE + 6, LANES),
            out_f32(3 * SIDE, LANES),
            own_shape,
            plane,
            out_f32(3, 16, LANES),
            out_f32(6, LANES),
        ),
        (cam_jac, jac, place, left, own, mate, other, inverse, given, state),
        scratch(6),
    )
    mate, other = exchange(to_mate, to_other)
    (left,) = call(early_kernel, (plane,), (jac, place, errors, own, mate, inverse))
    values, dots = call(
        sum_kernel, (own_shape, out_f32(chips, LANES)), (own, mate, other, inverse, rows)
    )
    dots = lax.all_to_all(dots, "chip", 0, 0, tiled=True)
    return call(
        finish_kernel,
        (out_f32(9, 16), out_f32(9, 16)),
        (cam_jac, jac, place, left, values, given, state, tilde, dots),
        [pltpu.VMEM((2, LANES, LANES), F32)],
    )


def solution(mesh):
    finer = Mesh(mesh.devices.reshape(-1, 2), SEG)
    return jax.shard_map(
        shards,
        mesh=finer,
        in_specs=(
            P(None, SEG, None),
            P(None, SEG, None),
            P(SEG, None),
            P(SEG),
            P(SEG, None),
            P(SEG, None),
            P(SEG),
            P(SEG),
            P(None, SEG),
            P(None, SEG),
        ),
        out_specs=(P(None, SEG), P(None, SEG)),
        check_vma=False,
    )
```

profile of v0, /device:TPU:1, one launch (start us, length us, event | category | flops | bytes accessed | tf_op | source)
XLA Modules:
  0.0 63.1 jit_solution(2004860444926320)
XLA Ops:
  0.6 0.0 copy-start
  0.6 3.5 %shard_map.113 = (f32[54,128]{1,0:T(8,128)S(1)}, f32[54,128]{1,0:T(8,128)S(1)}, f32[9,16,128]{2,1,0:T(8,128)S(1)}, s32[16,512]{1,0:T(8,128)S(1)}, f32[2,16,512]{...) custom-call(bf16[18,16,512]{2,1,0:T(8,128)(2,1)} %cam_ref.7, bf16[6,16,512]{2,1,0:T(8,128)(2,1)} %point_hbm.1, ...), custom_call_target="tpu_custom_call" | custom-call | tf_op jit(solution)/shard_map/pallas_call | solution.py:585
  4.1 3.3 %collective-permute-start = (f32[54,128]{1,0:T(8,128)S(1)}, f32[54,128]{1,0:T(8,128)S(1)}, u32[]{:S(2)}, u32[]{:S(2)}) collective-permute-start(f32[54,128]{1,0:T(8,128)S(1)} %get-tuple-element.27), channel_id=1, source_target_pairs={{0,1},{1,0},{2,3},{3,2},{4,5},{5,4},{6,7},{7,6},{8,9},{9,8},{10,11... | collective-permute-start | bytes 82952 | tf_op jit(solution)/shard_map/ppermute | solution.py:581
  7.4 1.9 %collective-permute-start.1 = (f32[54,128]{1,0:T(8,128)S(1)}, f32[54,128]{1,0:T(8,128)S(1)}, u32[]{:S(2)}, u32[]{:S(2)}) collective-permute-start(f32[54,128]{1,0:T(8,128)S(1)} %get-tuple-element.28), channel_id=1, source_target_pairs={{1,2},{2,1},{3,4},{4,3},{5,6},{6,5},{7,8},{8,7},{9,10},{10,9},{11,... | collective-permute-start | bytes 82952 | tf_op jit(solution)/shard_map/ppermute | solution.py:580
  9.3 0.0 copy-done
  9.4 0.1 shard_map.115.precond_in
  9.5 0.0 collective-permute-done.mate_in
  9.5 0.3 shard_map.114.errors_in
  9.8 2.8 %collective-permute-done.1.other_in = f32[54,128]{1,0:T(8,128)S(1)} collective-permute-done((f32[54,128]{1,0:T(8,128)S(1)}, f32[54,128]{1,0:T(8,128)S(1)}, u32[]{:S(2)}, u32[]{:S(2)}) %collective-permute-start.1) | collective-permute-done | bytes 27680 | tf_op jit(solution)/shard_map/ppermute | solution.py:580
  12.6 1.3 %shard_map.116 = (f32[18,128]{1,0:T(8,128)S(1)}, f32[18,128]{1,0:T(8,128)S(1)}, f32[3,16,128]{2,1,0:T(8,128)S(1)}, f32[2,16,512]{2,1,0:T(8,128)S(1)}, f32[6,16,1...) custom-call(bf16[18,16,512]{2,1,0:T(8,128)(2,1)S(1)} %copy-done, f32[7,16,512]{2,1,0:T(8,128)S(1)} %get-tuple-element.23.jac_ref, ...), custom_call_target="tpu_custom_call" | custom-call | tf_op jit(solution)/shard_map/pallas_call | solution.py:585
  14.0 0.1 collective-permute-start.2
  14.1 2.0 %collective-permute-start.3 = (f32[18,128]{1,0:T(8,128)S(1)}, f32[18,128]{1,0:T(8,128)S(1)}, u32[]{:S(2)}, u32[]{:S(2)}) collective-permute-start(f32[18,128]{1,0:T(8,128)S(1)} %get-tuple-element.34), channel_id=1, source_target_pairs={{1,2},{2,1},{3,4},{4,3},{5,6},{6,5},{7,8},{8,7},{9,10},{10,9},{11,... | collective-permute-start | bytes 27656 | tf_op jit(solution)/shard_map/ppermute | solution.py:580
  16.1 0.0 collective-permute-done.2.mate_in
  16.1 0.3 shard_map.117.errors_in
  16.4 2.7 %collective-permute-done.3.other_in = f32[18,128]{1,0:T(8,128)S(1)} collective-permute-done((f32[18,128]{1,0:T(8,128)S(1)}, f32[18,128]{1,0:T(8,128)S(1)}, u32[]{:S(2)}, u32[]{:S(2)}) %collective-permute-start.3) | collective-permute-done | bytes 9248 | tf_op jit(solution)/shard_map/ppermute | solution.py:580
  19.1 1.4 %shard_map.118 = (f32[24,128]{1,0:T(8,128)S(1)}, f32[18,128]{1,0:T(8,128)S(1)}, f32[3,16,128]{2,1,0:T(8,128)S(1)}, f32[2,16,512]{2,1,0:T(8,128)S(1)}, f32[3,16,128]{2,1,0:T(8,128)S(1)}, /*index=5*/f32[6,128]{1,0:T(8,128)S(1)}) custom-call(bf16[18,16,512]{2,1,0:T(8,128)(2,1)S(1)} %copy-done, f32[7,16,512]{2,1,0:T(8,128)S(1)} %get-tuple-element.23.jac_ref, ...), custom_call_target="tpu_custom_call" | custom-call | tf_op jit(solution)/shard_map/pallas_call | solution.py:585
  20.4 0.1 collective-permute-start.4
  20.5 2.4 %collective-permute-start.5 = (f32[18,128]{1,0:T(8,128)S(1)}, f32[18,128]{1,0:T(8,128)S(1)}, u32[]{:S(2)}, u32[]{:S(2)}) collective-permute-start(f32[18,128]{1,0:T(8,128)S(1)} %get-tuple-element.39), channel_id=1, source_target_pairs={{1,2},{2,1},{3,4},{4,3},{5,6},{6,5},{7,8},{8,7},{9,10},{10,9},{11,... | collective-permute-start | bytes 27656 | tf_op jit(solution)/shard_map/ppermute | solution.py:580
  22.9 2.6 %collective-permute-done.5.other_in = f32[18,128]{1,0:T(8,128)S(1)} collective-permute-done((f32[18,128]{1,0:T(8,128)S(1)}, f32[18,128]{1,0:T(8,128)S(1)}, u32[]{:S(2)}, u32[]{:S(2)}) %collective-permute-start.5) | collective-permute-done | bytes 9248 | tf_op jit(solution)/shard_map/ppermute | solution.py:580
  25.5 0.0 collective-permute-done.4.mate_in
  25.5 0.7 %shard_map.120 = (f32[3,16,128]{2,1,0:T(8,128)S(1)}, f32[128,128]{1,0:T(8,128)}) custom-call(f32[3,16,128]{2,1,0:T(8,128)S(1)} %get-tuple-element.37.own_in, f32[24,128]{1,0:T(8,128)S(1)} %collective-permute-done.4.mate_in, f32[18,128]{1,0:T(8,128)S(1)} %collective-permute-done.5.other_in, f32[6,16,128]{2,1,0:T(8,128)S(1)} %get-tuple-element.33.inverse_in, ...), custom_call_target="tpu_custom_call" | custom-call | tf_op jit(solution)/shard_map/pallas_call | solution.py:585
  26.3 24.9 %all-to-all-start = ((f32[128,1,128]{2,1,0:T(1,128)}), f32[128,1,128]{2,1,0:T(1,128)S(1)}, u32[]{:S(2)}, u32[]{:S(2)}) async-start(f32[128,1,128]{2,1,0:T(1,128)} %bitcast.4), calls=%async_computation | async-start | bytes 131072 | tf_op jit(solution)/shard_map/all_to_all | solution.py:649
  51.2 0.3 shard_map.119.errors_in
  51.6 10.3 %all-to-all-done = f32[128,1,128]{2,1,0:T(1,128)S(1)} async-done(((f32[128,1,128]{2,1,0:T(1,128)}), f32[128,1,128]{2,1,0:T(1,128)S(1)}, u32[]{:S(2)}, u32[]{:S(2)}) %all-to-all-start) | async-done | bytes 65568 | tf_op jit(solution)/shard_map/all_to_all | solution.py:649
  61.8 1.2 %shard_map.121 = (f32[9,16]{1,0:T(8,128)}, f32[9,16]{1,0:T(8,128)}) custom-call(bf16[18,16,512]{2,1,0:T(8,128)(2,1)S(1)} %copy-done, f32[7,16,512]{2,1,0:T(8,128)S(1)} %get-tuple-element.23.jac_ref, s32[16,512]{1,0:T(8,128)S(1)} %get-tuple-element.24.index_ref, f32[2,16,512]{2,1,0:T(8,128)S(1)} %shard_map.119.errors_in, ...), custom_call_target="tpu_custom_call" | custom-call | tf_op jit(solution)/shard_map/pallas_call | solution.py:585
Async XLA Ops:
  0.6 8.7 %copy-start = (bf16[18,16,512]{2,1,0:T(8,128)(2,1)S(1)}, bf16[18,16,512]{2,1,0:T(8,128)(2,1)}, u32[]{:S(2)}) copy-start(bf16[18,16,512]{2,1,0:T(8,128)(2,1)} %cam_ref.7) | copy-start | bytes 884740
  4.1 5.4 %collective-permute-start = (f32[54,128]{1,0:T(8,128)S(1)}, f32[54,128]{1,0:T(8,128)S(1)}, u32[]{:S(2)}, u32[]{:S(2)}) collective-permute-start(f32[54,128]{1,0:T(8,128)S(1)} %get-tuple-element.27), channel_id=1, source_target_pairs={{0,1},{1,0},{2,3},{3,2},{4,5},{5,4},{6,7},{7,6},{8,9},{9,8},{10,11... | collective-permute-start | bytes 82952 | tf_op jit(solution)/shard_map/ppermute | solution.py:581
  7.4 5.2 %collective-permute-start.1 = (f32[54,128]{1,0:T(8,128)S(1)}, f32[54,128]{1,0:T(8,128)S(1)}, u32[]{:S(2)}, u32[]{:S(2)}) collective-permute-start(f32[54,128]{1,0:T(8,128)S(1)} %get-tuple-element.28), channel_id=1, source_target_pairs={{1,2},{2,1},{3,4},{4,3},{5,6},{6,5},{7,8},{8,7},{9,10},{10,9},{11,... | collective-permute-start | bytes 82952 | tf_op jit(solution)/shard_map/ppermute | solution.py:580
  14.0 2.1 %collective-permute-start.2 = (f32[18,128]{1,0:T(8,128)S(1)}, f32[18,128]{1,0:T(8,128)S(1)}, u32[]{:S(2)}, u32[]{:S(2)}) collective-permute-start(f32[18,128]{1,0:T(8,128)S(1)} %get-tuple-element.32), channel_id=1, source_target_pairs={{0,1},{1,0},{2,3},{3,2},{4,5},{5,4},{6,7},{7,6},{8,9},{9,8},{10,11... | collective-permute-start | bytes 27656 | tf_op jit(solution)/shard_map/ppermute | solution.py:581
  14.1 5.0 %collective-permute-start.3 = (f32[18,128]{1,0:T(8,128)S(1)}, f32[18,128]{1,0:T(8,128)S(1)}, u32[]{:S(2)}, u32[]{:S(2)}) collective-permute-start(f32[18,128]{1,0:T(8,128)S(1)} %get-tuple-element.34), channel_id=1, source_target_pairs={{1,2},{2,1},{3,4},{4,3},{5,6},{6,5},{7,8},{8,7},{9,10},{10,9},{11,... | collective-permute-start | bytes 27656 | tf_op jit(solution)/shard_map/ppermute | solution.py:580
  20.4 5.1 %collective-permute-start.4 = (f32[24,128]{1,0:T(8,128)S(1)}, f32[24,128]{1,0:T(8,128)S(1)}, u32[]{:S(2)}, u32[]{:S(2)}) collective-permute-start(f32[24,128]{1,0:T(8,128)S(1)} %get-tuple-element.38), channel_id=1, source_target_pairs={{0,1},{1,0},{2,3},{3,2},{4,5},{5,4},{6,7},{7,6},{8,9},{9,8},{10,11... | collective-permute-start | bytes 36872 | tf_op jit(solution)/shard_map/ppermute | solution.py:581
  20.5 5.0 %collective-permute-start.5 = (f32[18,128]{1,0:T(8,128)S(1)}, f32[18,128]{1,0:T(8,128)S(1)}, u32[]{:S(2)}, u32[]{:S(2)}) collective-permute-start(f32[18,128]{1,0:T(8,128)S(1)} %get-tuple-element.39), channel_id=1, source_target_pairs={{1,2},{2,1},{3,4},{4,3},{5,6},{6,5},{7,8},{8,7},{9,10},{10,9},{11,... | collective-permute-start | bytes 27656 | tf_op jit(solution)/shard_map/ppermute | solution.py:580
  26.3 35.5 %all-to-all-start = ((f32[128,1,128]{2,1,0:T(1,128)}), f32[128,1,128]{2,1,0:T(1,128)S(1)}, u32[]{:S(2)}, u32[]{:S(2)}) async-start(f32[128,1,128]{2,1,0:T(1,128)} %bitcast.4), calls=%async_computation | async-start | bytes 131072 | tf_op jit(solution)/shard_map/all_to_all | solution.py:649
where the time goes:
time: 63.3 us; the launch traced here: 63.1 us
  starting transfers between devices  34.7 us (55%)
  waiting for transfers between devices  18.3 us (29%)
  Pallas kernels  9.25 us (15%)
  between operations  0.76 us (1%)
    all_to_all x1, starting transfers between devices, shards(): dots = lax.all_to_all(dots, 'chip', 0, 0, tiled=True)  24.9 us
    all_to_all x1, waiting for transfers between devices, shards(): dots = lax.all_to_all(dots, 'chip', 0, 0, tiled=True)  10.3 us
    pallas_call x9, Pallas kernels, call(): pl.pallas_call(kernel, out_shape=outs, in_specs=spaces or vmem(len(operan...  9.25 us
    ppermute x3, waiting for transfers between devices, exchange(): other = lax.ppermute(to_other, SEG, others)  8.06 us
    ppermute x3, starting transfers between devices, exchange(): other = lax.ppermute(to_other, SEG, others)  6.3 us
    ppermute x3, starting transfers between devices, exchange(): mate = lax.ppermute(to_mate, SEG, mates)  3.47 us
  transfers between devices with their start and end apart: 7, of which 4 were waited for; matrix products, arithmetic and copies ran while one was open for 0% of the time, Pallas kernels for 2%

commit v1 on v0

--- a/solution.py
+++ b/solution.py
@@ -163,9 +163,9 @@
 def first_kernel(
     cam_hbm, point_hbm, obs_hbm, count_hbm, back_hbm, front_hbm, damp_hbm, cam_damp_hbm,
     right_hbm, guess_hbm,
-    mate_ref, other_ref, own_ref, index_ref, errors_ref, jac_ref, state_ref,
+    mate_ref, other_ref, own_ref, index_ref, errors_ref, jac_ref, state_ref, cam_ref,
     value_ref, high_ref, low_ref,
-    cam_ref, point_ref, obs_ref, count_ref, back_ref, front_ref, damp_ref, cam_damp_ref,
+    point_ref, obs_ref, count_ref, back_ref, front_ref, damp_ref, cam_damp_ref,
     right_ref, guess_ref, flip_ref, sems,
 ):
     sources = (
@@ -188,8 +188,7 @@
     for copy in copies[:2]:
         copy.wait()
     table = point_table(back_ref[...], front_ref[...])
-    for copy in copies[2:7]:
-        copy.wait()
+    copies[2].wait()
     observed = obs_ref[...]
     own_place = gather_rows([table], observed >> 7, observed & 127, points // LANES)[0]
     place = jnp.where(
@@ -205,6 +204,8 @@
     high_ref[...] = (place >> 7).astype(F32)
     low_ref[...] = (place & 127).astype(F32)
     valid = lane_iota(16, LANES) < 9
+    for copy in copies[3:7]:
+        copy.wait()
     flip_ref[0, :9, :16] = guess_ref[...]
     flip_ref[1, :9, :16] = right_ref[...]
     flip_ref[2, 0:1, :16] = cam_damp_ref[...]
@@ -592,7 +593,7 @@
         )(*operands)
 
     plane = out_f32(2, cameras, width)
-    to_mate, to_other, own, place, errors, jac, given = call(
+    to_mate, to_other, own, place, errors, jac, given, cam_jac = call(
         first_kernel,
         (
             out_f32(9 * SIDE, LANES),
@@ -602,10 +603,11 @@
             plane,
             out_f32(7, cameras, width),
             out_f32(3, 16, LANES),
+            jax.ShapeDtypeStruct(cam_jac.shape, cam_jac.dtype),
         ),
         tuple(pltpu.with_memory_space_constraint(value, pltpu.HBM) for value in inputs),
         scratch(18)
-        + [pltpu.VMEM(value.shape, value.dtype) for value in inputs]
+        + [pltpu.VMEM(value.shape, value.dtype) for value in inputs[1:]]
         + [pltpu.VMEM((3, LANES, LANES), F32), pltpu.SemaphoreType.DMA((len(inputs),))],
         [pl.BlockSpec(memory_space=pltpu.HBM) for _ in inputs],
     )

time: 63.3 us -> 63.4 us (level)
  no operation moved by 1% of the time
where the time goes in v1:
time: 63.4 us; the launch traced here: 63.1 us
  starting transfers between devices  34.7 us (55%)
  waiting for transfers between devices  18.4 us (29%)
  Pallas kernels  9.33 us (15%)
  between operations  0.74 us (1%)
    all_to_all x1, starting transfers between devices, shards(): dots = lax.all_to_all(dots, 'chip', 0, 0, tiled=True)  24.9 us
    all_to_all x1, waiting for transfers between devices, shards(): dots = lax.all_to_all(dots, 'chip', 0, 0, tiled=True)  10.3 us
    pallas_call x9, Pallas kernels, call(): pl.pallas_call(kernel, out_shape=outs, in_specs=spaces or vmem(len(operan...  9.33 us
    ppermute x3, waiting for transfers between devices, exchange(): other = lax.ppermute(to_other, SEG, others)  8.07 us
    ppermute x3, starting transfers between devices, exchange(): other = lax.ppermute(to_other, SEG, others)  6.3 us
    ppermute x3, starting transfers between devices, exchange(): mate = lax.ppermute(to_mate, SEG, mates)  3.47 us
  transfers between devices with their start and end apart: 7, of which 4 were waited for; matrix products, arithmetic and copies ran while one was open for 0% of the time, Pallas kernels for 2%

profile of v1, /device:TPU:1, one launch (start us, length us, event | category | flops | bytes accessed | tf_op | source)
XLA Modules:
  0.0 63.1 jit_solution(8141565180455015146)
XLA Ops:
  0.6 3.6 %shard_map.113 = (f32[54,128]{1,0:T(8,128)S(1)}, f32[54,128]{1,0:T(8,128)S(1)}, f32[9,16,128]{2,1,0:T(8,128)S(1)}, s32[16,512]{1,0:T(8,128)S(1)}, f32[2,16,512]{...) custom-call(bf16[18,16,512]{2,1,0:T(8,128)(2,1)} %cam_hbm.1, ...), custom_call_target="tpu_custom_call" | custom-call | tf_op jit(solution)/shard_map/pallas_call | solution.py:586
  4.2 3.3 %collective-permute-start = (f32[54,128]{1,0:T(8,128)S(1)}, f32[54,128]{1,0:T(8,128)S(1)}, u32[]{:S(2)}, u32[]{:S(2)}) collective-permute-start(f32[54,128]{1,0:T(8,128)S(1)} %get-tuple-element.29), channel_id=1, source_target_pairs={{0,1},{1,0},{2,3},{3,2},{4,5},{5,4},{6,7},{7,6},{8,9},{9,8},{10,11... | collective-permute-start | bytes 82952 | tf_op jit(solution)/shard_map/ppermute | solution.py:582
  7.5 1.9 %collective-permute-start.1 = (f32[54,128]{1,0:T(8,128)S(1)}, f32[54,128]{1,0:T(8,128)S(1)}, u32[]{:S(2)}, u32[]{:S(2)}) collective-permute-start(f32[54,128]{1,0:T(8,128)S(1)} %get-tuple-element.30), channel_id=1, source_target_pairs={{1,2},{2,1},{3,4},{4,3},{5,6},{6,5},{7,8},{8,7},{9,10},{10,9},{11,... | collective-permute-start | bytes 82952 | tf_op jit(solution)/shard_map/ppermute | solution.py:581
  9.4 0.1 shard_map.115.precond_in
  9.6 0.0 collective-permute-done.mate_in
  9.6 0.3 shard_map.114.errors_in
  9.9 2.8 %collective-permute-done.1.other_in = f32[54,128]{1,0:T(8,128)S(1)} collective-permute-done((f32[54,128]{1,0:T(8,128)S(1)}, f32[54,128]{1,0:T(8,128)S(1)}, u32[]{:S(2)}, u32[]{:S(2)}) %collective-permute-start.1) | collective-permute-done | bytes 27680 | tf_op jit(solution)/shard_map/ppermute | solution.py:581
  12.7 1.3 %shard_map.116 = (f32[18,128]{1,0:T(8,128)S(1)}, f32[18,128]{1,0:T(8,128)S(1)}, f32[3,16,128]{2,1,0:T(8,128)S(1)}, f32[2,16,512]{2,1,0:T(8,128)S(1)}, f32[6,16,1...) custom-call(bf16[18,16,512]{2,1,0:T(8,128)(2,1)S(1)} %get-tuple-element.24.cam_ref, ...), custom_call_target="tpu_custom_call" | custom-call | tf_op jit(solution)/shard_map/pallas_call | solution.py:586
  14.0 0.1 collective-permute-start.2
  14.1 2.0 %collective-permute-start.3 = (f32[18,128]{1,0:T(8,128)S(1)}, f32[18,128]{1,0:T(8,128)S(1)}, u32[]{:S(2)}, u32[]{:S(2)}) collective-permute-start(f32[18,128]{1,0:T(8,128)S(1)} %get-tuple-element.36), channel_id=1, source_target_pairs={{1,2},{2,1},{3,4},{4,3},{5,6},{6,5},{7,8},{8,7},{9,10},{10,9},{11,... | collective-permute-start | bytes 27656 | tf_op jit(solution)/shard_map/ppermute | solution.py:581
  16.2 0.0 collective-permute-done.2.mate_in
  16.2 0.3 shard_map.117.errors_in
  16.5 2.7 %collective-permute-done.3.other_in = f32[18,128]{1,0:T(8,128)S(1)} collective-permute-done((f32[18,128]{1,0:T(8,128)S(1)}, f32[18,128]{1,0:T(8,128)S(1)}, u32[]{:S(2)}, u32[]{:S(2)}) %collective-permute-start.3) | collective-permute-done | bytes 9248 | tf_op jit(solution)/shard_map/ppermute | solution.py:581
  19.2 1.4 %shard_map.118 = (f32[24,128]{1,0:T(8,128)S(1)}, f32[18,128]{1,0:T(8,128)S(1)}, f32[3,16,128]{2,1,0:T(8,128)S(1)}, f32[2,16,512]{2,1,0:T(8,128)S(1)}, f32[3,16,128]{2,1,0:T(8,128)S(1)}, /*index=5*/f32[6,128]{1,0:T(8,128)S(1)}) custom-call(bf16[18,16,512]{2,1,0:T(8,128)(2,1)S(1)} %get-tuple-element.24.cam_ref, f32[7,16,512]{2,1,0:T(8,128)S(1)} %get-tuple-element.25.jac_ref, ...), custom_call_target="tpu_custom_call" | custom-call | tf_op jit(solution)/shard_map/pallas_call | solution.py:586
  20.5 0.1 collective-permute-start.4
  20.6 2.4 %collective-permute-start.5 = (f32[18,128]{1,0:T(8,128)S(1)}, f32[18,128]{1,0:T(8,128)S(1)}, u32[]{:S(2)}, u32[]{:S(2)}) collective-permute-start(f32[18,128]{1,0:T(8,128)S(1)} %get-tuple-element.41), channel_id=1, source_target_pairs={{1,2},{2,1},{3,4},{4,3},{5,6},{6,5},{7,8},{8,7},{9,10},{10,9},{11,... | collective-permute-start | bytes 27656 | tf_op jit(solution)/shard_map/ppermute | solution.py:581
  23.0 2.6 %collective-permute-done.5.other_in = f32[18,128]{1,0:T(8,128)S(1)} collective-permute-done((f32[18,128]{1,0:T(8,128)S(1)}, f32[18,128]{1,0:T(8,128)S(1)}, u32[]{:S(2)}, u32[]{:S(2)}) %collective-permute-start.5) | collective-permute-done | bytes 9248 | tf_op jit(solution)/shard_map/ppermute | solution.py:581
  25.6 0.0 collective-permute-done.4.mate_in
  25.6 0.7 %shard_map.120 = (f32[3,16,128]{2,1,0:T(8,128)S(1)}, f32[128,128]{1,0:T(8,128)}) custom-call(f32[3,16,128]{2,1,0:T(8,128)S(1)} %get-tuple-element.39.own_in, f32[24,128]{1,0:T(8,128)S(1)} %collective-permute-done.4.mate_in, f32[18,128]{1,0:T(8,128)S(1)} %collective-permute-done.5.other_in, f32[6,16,128]{2,1,0:T(8,128)S(1)} %get-tuple-element.35.inverse_in, ...), custom_call_target="tpu_custom_call" | custom-call | tf_op jit(solution)/shard_map/pallas_call | solution.py:586
  26.4 24.9 %all-to-all-start = ((f32[128,1,128]{2,1,0:T(1,128)}), f32[128,1,128]{2,1,0:T(1,128)S(1)}, u32[]{:S(2)}, u32[]{:S(2)}) async-start(f32[128,1,128]{2,1,0:T(1,128)} %bitcast.4), calls=%async_computation | async-start | bytes 131072 | tf_op jit(solution)/shard_map/all_to_all | solution.py:651
  51.3 0.3 shard_map.119.errors_in
  51.6 10.3 %all-to-all-done = f32[128,1,128]{2,1,0:T(1,128)S(1)} async-done(((f32[128,1,128]{2,1,0:T(1,128)}), f32[128,1,128]{2,1,0:T(1,128)S(1)}, u32[]{:S(2)}, u32[]{:S(2)}) %all-to-all-start) | async-done | bytes 65568 | tf_op jit(solution)/shard_map/all_to_all | solution.py:651
  61.9 1.2 %shard_map.121 = (f32[9,16]{1,0:T(8,128)}, f32[9,16]{1,0:T(8,128)}) custom-call(bf16[18,16,512]{2,1,0:T(8,128)(2,1)S(1)} %get-tuple-element.24.cam_ref, f32[7,16,512]{2,1,0:T(8,128)S(1)} %get-tuple-element.25.jac_ref, s32[16,512]{1,0:T(8,128)S(1)} %get-tuple-element.26.index_ref, f32[2,16,512]{2,1,0:T(8,128)S(1)} %shard_map.119.errors_in, ...), custom_call_target="tpu_custom_call" | custom-call | tf_op jit(solution)/shard_map/pallas_call | solution.py:586
Async XLA Ops:
  4.2 5.4 %collective-permute-start = (f32[54,128]{1,0:T(8,128)S(1)}, f32[54,128]{1,0:T(8,128)S(1)}, u32[]{:S(2)}, u32[]{:S(2)}) collective-permute-start(f32[54,128]{1,0:T(8,128)S(1)} %get-tuple-element.29), channel_id=1, source_target_pairs={{0,1},{1,0},{2,3},{3,2},{4,5},{5,4},{6,7},{7,6},{8,9},{9,8},{10,11... | collective-permute-start | bytes 82952 | tf_op jit(solution)/shard_map/ppermute | solution.py:582
  7.5 5.2 %collective-permute-start.1 = (f32[54,128]{1,0:T(8,128)S(1)}, f32[54,128]{1,0:T(8,128)S(1)}, u32[]{:S(2)}, u32[]{:S(2)}) collective-permute-start(f32[54,128]{1,0:T(8,128)S(1)} %get-tuple-element.30), channel_id=1, source_target_pairs={{1,2},{2,1},{3,4},{4,3},{5,6},{6,5},{7,8},{8,7},{9,10},{10,9},{11,... | collective-permute-start | bytes 82952 | tf_op jit(solution)/shard_map/ppermute | solution.py:581
  14.0 2.1 %collective-permute-start.2 = (f32[18,128]{1,0:T(8,128)S(1)}, f32[18,128]{1,0:T(8,128)S(1)}, u32[]{:S(2)}, u32[]{:S(2)}) collective-permute-start(f32[18,128]{1,0:T(8,128)S(1)} %get-tuple-element.34), channel_id=1, source_target_pairs={{0,1},{1,0},{2,3},{3,2},{4,5},{5,4},{6,7},{7,6},{8,9},{9,8},{10,11... | collective-permute-start | bytes 27656 | tf_op jit(solution)/shard_map/ppermute | solution.py:582
  14.1 5.0 %collective-permute-start.3 = (f32[18,128]{1,0:T(8,128)S(1)}, f32[18,128]{1,0:T(8,128)S(1)}, u32[]{:S(2)}, u32[]{:S(2)}) collective-permute-start(f32[18,128]{1,0:T(8,128)S(1)} %get-tuple-element.36), channel_id=1, source_target_pairs={{1,2},{2,1},{3,4},{4,3},{5,6},{6,5},{7,8},{8,7},{9,10},{10,9},{11,... | collective-permute-start | bytes 27656 | tf_op jit(solution)/shard_map/ppermute | solution.py:581
  20.5 5.1 %collective-permute-start.4 = (f32[24,128]{1,0:T(8,128)S(1)}, f32[24,128]{1,0:T(8,128)S(1)}, u32[]{:S(2)}, u32[]{:S(2)}) collective-permute-start(f32[24,128]{1,0:T(8,128)S(1)} %get-tuple-element.40), channel_id=1, source_target_pairs={{0,1},{1,0},{2,3},{3,2},{4,5},{5,4},{6,7},{7,6},{8,9},{9,8},{10,11... | collective-permute-start | bytes 36872 | tf_op jit(solution)/shard_map/ppermute | solution.py:582
  20.6 5.0 %collective-permute-start.5 = (f32[18,128]{1,0:T(8,128)S(1)}, f32[18,128]{1,0:T(8,128)S(1)}, u32[]{:S(2)}, u32[]{:S(2)}) collective-permute-start(f32[18,128]{1,0:T(8,128)S(1)} %get-tuple-element.41), channel_id=1, source_target_pairs={{1,2},{2,1},{3,4},{4,3},{5,6},{6,5},{7,8},{8,7},{9,10},{10,9},{11,... | collective-permute-start | bytes 27656 | tf_op jit(solution)/shard_map/ppermute | solution.py:581
  26.4 35.6 %all-to-all-start = ((f32[128,1,128]{2,1,0:T(1,128)}), f32[128,1,128]{2,1,0:T(1,128)S(1)}, u32[]{:S(2)}, u32[]{:S(2)}) async-start(f32[128,1,128]{2,1,0:T(1,128)} %bitcast.4), calls=%async_computation | async-start | bytes 131072 | tf_op jit(solution)/shard_map/all_to_all | solution.py:651
